TPU v7x, 32 devices: a whole 2x2x4 slice. The times are simulated.
32 devices in a mesh: node: 4 (over x, core), sx: 2 (over y), sy: 4 (over z).
Axes of the slice: x: 2, y: 2, z: 4, core: 2. Of those that a mesh axis runs over, the one named last changes fastest.
Arguments:
- previous: float32 [4, 2, 32, 128, 256], P('node', None, 'sx', 'sy'), may hold values from 0 to 1
- feed_rate: float32 [32, 128, 256], P('sx', 'sy'), may hold values from 0.01 to 0.1
- kill_rate: float32 [32, 128, 256], P('sx', 'sy'), may hold values from 0.03 to 0.1
Outputs:
- sections: float32 [4, 2, 32, 128, 256], P('node', None, 'sx', 'sy')
All inputs are finite; a program needn't handle non-finite values.
Results may differ from a plain program's by a relative error of at most 0.00011.
Values sent between devices are 32-bit elements; how exact they have to be, the bound alone decides.
A program may use at most 64 MiB of HBM per device.

v0:
```python
import jax
import jax.numpy as jnp
from jax import lax
from jax.sharding import PartitionSpec as P

SWEEPS = 2
JACOBI = 12


radau_points = [0.088587959512704, 0.409466864440735, 0.787659461760847, 1.0]
time_step = 4.0
diffusion_values = [1.0, 0.5]


def from_root(value, axis, source):
    kept = jnp.where(lax.axis_index(axis) == source, value, 0).astype(value.dtype)
    return lax.psum(kept, axis)


def padded_2(block, sides, width):
    for axis, dim in sides:
        count = lax.axis_size(axis)
        forward = [(i, i + 1) for i in range(count - 1)]
        forward.append((count - 1, 0))
        backward = [(target, source) for source, target in forward]
        low = lax.ppermute(
            lax.slice_in_dim(block, block.shape[dim] - width, None, axis=dim), axis, forward
        )
        high = lax.ppermute(lax.slice_in_dim(block, 0, width, axis=dim), axis, backward)
        block = jnp.concatenate([low, block, high], axis=dim)
    return block


def collocation():
    count = len(radau_points)
    table = []
    for row in range(count):
        table.append([0.0] * count)
    for column in range(count):
        poly = [1.0]
        denom = 1.0
        for other in range(count):
            if other != column:
                longer = [0.0] * (len(poly) + 1)
                for place in range(len(poly)):
                    longer[place + 1] = longer[place + 1] + poly[place]
                    longer[place] = longer[place] - radau_points[other] * poly[place]
                poly = longer
                denom = denom * (radau_points[column] - radau_points[other])
        for row in range(count):
            point = radau_points[row]
            total = 0.0
            for place in range(len(poly)):
                total = total + poly[place] * point ** (place + 1) / (place + 1)
            table[row][column] = total / denom
    return table


def beside(padded):
    center = padded[:, 1:-1, 1:-1]
    total = padded[:, 2:, 1:-1] + padded[:, :-2, 1:-1]
    total = total + padded[:, 1:-1, 2:] + padded[:, 1:-1, :-2]
    return total + jnp.roll(center, 1, 3) + jnp.roll(center, -1, 3)


def body(previous, feed_rate, kill_rate):
    node_index = lax.axis_index("node")
    qmatrix = jnp.asarray(collocation(), jnp.float32)
    points = jnp.asarray(radau_points, jnp.float32)
    diag_weight = points[node_index]
    diffusion = jnp.asarray(diffusion_values, jnp.float32)[:, None, None, None]
    coef = time_step * diag_weight * diffusion
    start_value = from_root(previous[0], "node", len(radau_points) - 1)
    iterate = previous[0]
    for sweep in range(SWEEPS):
        padded = padded_2(iterate, (("sx", 1), ("sy", 2)), 1)
        diff = diffusion * (beside(padded) - 6.0 * iterate)
        upart = iterate[0]
        vpart = iterate[1]
        uvv = upart * vpart * vpart
        react = jnp.stack(
            [-uvv + feed_rate * (1.0 - upart), uvv - (feed_rate + kill_rate) * vpart], 0
        )
        force = diff + react
        weights = qmatrix[:, node_index][:, None, None, None, None]
        section_terms = weights * force[None]
        summed = lax.psum_scatter(section_terms, "node", scatter_dimension=0, tiled=True)[0]
        right_side = start_value + time_step * (summed - diag_weight * diff)
        extended = padded_2(right_side, (("sx", 1), ("sy", 2)), 1)

        def double_turn(turn, current):
            beside_all = padded_2(current, (("sx", 1), ("sy", 2)), 2)
            midway = (extended + coef * beside(beside_all)) / (1.0 + 6.0 * coef)
            return (right_side + coef * beside(midway)) / (1.0 + 6.0 * coef)

        iterate = lax.fori_loop(0, JACOBI // 2, double_turn, iterate)
    return iterate[None]


def solution(mesh):
    return jax.shard_map(
        body,
        mesh=mesh,
        in_specs=(P("node", None, "sx", "sy", None), P("sx", "sy", None), P("sx", "sy", None)),
        out_specs=P("node", None, "sx", "sy", None),
        check_vma=False,
    )
```

profile of v0, /device:TPU:0, one launch (start us, length us, event | category | flops | bytes accessed | tf_op | source)
XLA Modules:
  0.0 408.7 jit_solution(10486807941716206749)
XLA Ops:
  7.8 3.1 collective-permute-start.9
  16.1 4.1 collective-permute-start.10
  21.9 4.1 %collective-permute-done.11 = f32[2,18,1,256]{3,2,1,0:T(1,128)S(1)} collective-permute-done((f32[2,18,1,256]{3,2,1,0:T(1,128)S(1)}, f32[2,18,1,256]{3,2,1,0:T(1,128)S(1)}, u32[]{:S(2)}, u32[]{:S(2)}) %collective-permute-start.11) | collective-permute-done | bytes 36896 | tf_op jit(solution)/shard_map/ppermute | solution.py:26
  28.3 2.6 broadcast_multiply_fusion.3
  32.2 18.0 %all-reduce.2.cloned.1.call-done = f32[2,16,32,256]{3,2,1,0:T(8,128)} async-done(((f32[2,16,32,256]{3,2,1,0:T(8,128)}), f32[2,16,32,256]{3,2,1,0:T(8,128)}) %all-reduce.2.cloned.1.call-update) | async-done | bytes 1048592 | tf_op jit(solution)/shard_map/psum | solution.py:17
  50.2 47.6 %reduce-scatter.3.cloned.1.call-done = f32[1,2,16,32,256]{4,3,2,1,0:T(8,128)} async-done(((f32[4,2,16,32,256]{4,3,2,1,0:T(8,128)}), f32[1,2,16,32,256]{4,3,2,1,0:T(8,128)}) %reduce-scatter.3.cloned.1.call-update) | async-done | bytes 1048592 | tf_op jit(solution)/shard_map/reduce_scatter | solution.py:87
  102.3 2.8 collective-permute-done.12
  113.4 106.2 %while.22 = (s32[]{:T(128)}, f32[2,16,32,256]{3,2,1,0:T(8,128)S(1)}, f32[2,18,34,256]{3,2,1,0:T(8,128)}, f32[2,16,32,256]{3,2,1,0:T(8,128)S(1)}, f32[]{:T(128)}, /*index=5*/s32[]{:T(128)}, f32[2]{0:T(128)S(1)}) while((s32[]{:T(128)}, f32[2,16,32,256]{3,2,1,0:T(8,128)S(1)}, f32[2,18,34,256]{3,2,1,0:T(8,128)}, ...), condition=%wide.region_3.4_spmd.clone, body=%wide.region_2.3_spmd.clone.sunk | while | flops 7118856 | bytes 39731524 | solution.py:96
  115.5 2.9 collective-permute-done
  121.0 2.7 collective-permute-start.3
  123.8 2.5 collective-permute-done.2
  132.9 2.9 collective-permute-done
  138.6 2.5 collective-permute-start.3
  141.2 2.5 collective-permute-done.2
  150.4 2.9 collective-permute-done
  156.0 2.7 collective-permute-start.3
  158.7 2.5 collective-permute-done.2
  167.8 2.9 collective-permute-done
  173.5 2.5 collective-permute-start.3
  176.1 2.5 collective-permute-done.2
  185.4 2.9 collective-permute-done
  190.9 2.7 collective-permute-start.3
  193.7 2.5 collective-permute-done.2
  202.8 2.9 collective-permute-done
  209.9 2.5 collective-permute-start.3
  222.3 2.9 collective-permute-done.17
  225.4 3.4 collective-permute-start.18
  230.5 4.1 %collective-permute-done.19 = f32[2,18,1,256]{3,2,1,0:T(1,128)S(1)} collective-permute-done((f32[2,18,1,256]{3,2,1,0:T(1,128)S(1)}, f32[2,18,1,256]{3,2,1,0:T(1,128)S(1)}, u32[]{:S(2)}, u32[]{:S(2)}) %collective-permute-start.19) | collective-permute-done | bytes 36896 | tf_op jit(solution)/shard_map/ppermute | solution.py:26
  236.4 2.6 broadcast_multiply_fusion.2
  239.1 41.7 %reduce-scatter.5.cloned.1.call-done = f32[1,2,16,32,256]{4,3,2,1,0:T(8,128)} async-done(((f32[4,2,16,32,256]{4,3,2,1,0:T(8,128)}), f32[1,2,16,32,256]{4,3,2,1,0:T(8,128)}) %reduce-scatter.5.cloned.1.call-update) | async-done | bytes 1048592 | tf_op jit(solution)/shard_map/reduce_scatter | solution.py:87
  285.4 2.8 collective-permute-done.20
  296.4 104.8 %while.23 = (s32[]{:T(128)}, f32[2,16,32,256]{3,2,1,0:T(8,128)S(1)}, f32[2,18,34,256]{3,2,1,0:T(8,128)}, f32[2,16,32,256]{3,2,1,0:T(8,128)S(1)}, f32[]{:T(128)}, /*index=5*/s32[]{:T(128)}, f32[2]{0:T(128)S(1)}) while((s32[]{:T(128)}, f32[2,16,32,256]{3,2,1,0:T(8,128)S(1)}, f32[2,18,34,256]{3,2,1,0:T(8,128)}, ...), condition=%wide.region_6.7_spmd.clone, body=%wide.region_5.6_spmd.clone.sunk | while | flops 7118856 | bytes 39731524 | solution.py:96
  298.5 2.9 collective-permute-done.4
  304.1 2.7 collective-permute-start.7
  306.8 2.5 collective-permute-done.6
  315.9 2.9 collective-permute-done.4
  321.7 2.6 collective-permute-start.7
  324.2 2.5 collective-permute-done.6
  333.5 2.9 collective-permute-done.4
  339.0 2.7 collective-permute-start.7
  341.8 2.5 collective-permute-done.6
  350.8 2.9 collective-permute-done.4
  356.6 2.6 collective-permute-start.7
  368.4 2.9 collective-permute-done.4
  374.0 2.7 collective-permute-start.7
  376.7 2.5 collective-permute-done.6
  385.8 2.9 collective-permute-done.4
  391.5 2.6 collective-permute-start.7
  (320 shorter events, 164.0 us)
Async XLA Ops:
  6.5 43.6 %all-reduce.2.cloned.1.call-start = ((), (), s32[]{:S(2)}) async-start(), calls=%async_computation.2 | async-start | bytes 2097152 | tf_op jit(solution)/shard_map/psum | solution.py:17
  7.8 8.3 %collective-permute-start.9 = (f32[2,1,32,256]{3,2,1,0:T(8,128)S(1)}, f32[2,1,32,256]{3,2,1,0:T(8,128)S(1)}, u32[]{:S(2)}, u32[]{:S(2)}) collective-permute-start(f32[2,1,32,256]{3,2,1,0:T(8,128)S(1)} %get-tuple-element.162), channel_id=1, source_target_pairs={{0,4},{4,0},{1,5},{5,1},{2,6},{6,2},{3,7},{7,3},{8,12},{12,8},{9,1... | collective-permute-start | bytes 196616 | tf_op jit(solution)/shard_map/ppermute | solution.py:26
  10.8 5.2 %collective-permute-start.8 = (f32[2,1,32,256]{3,2,1,0:T(8,128)S(1)}, f32[2,1,32,256]{3,2,1,0:T(8,128)S(1)}, u32[]{:S(2)}, u32[]{:S(2)}) collective-permute-start(f32[2,1,32,256]{3,2,1,0:T(8,128)S(1)} %get-tuple-element.163), channel_id=1, source_target_pairs={{4,0},{0,4},{5,1},{1,5},{6,2},{2,6},{7,3},{3,7},{12,8},{8,12},{13,... | collective-permute-start | bytes 196616 | tf_op jit(solution)/shard_map/ppermute | solution.py:29
  12.0 85.7 %reduce-scatter.3.cloned.1.call-start = ((), (), s32[]{:S(2)}) async-start(), calls=%async_computation.3 | async-start | bytes 5242880 | tf_op jit(solution)/shard_map/reduce_scatter | solution.py:87
  16.1 5.7 %collective-permute-start.10 = (f32[2,18,1,256]{3,2,1,0:T(1,128)S(1)}, f32[2,18,1,256]{3,2,1,0:T(1,128)S(1)}, u32[]{:S(2)}, u32[]{:S(2)}) collective-permute-start(f32[2,18,1,256]{3,2,1,0:T(1,128)S(1)} %get-tuple-element.148), channel_id=1, source_target_pairs={{1,0},{2,1},{3,2},{0,3},{5,4},{6,5},{7,6},{4,7},{9,8},{10,9},{11,1... | collective-permute-start | bytes 110600 | tf_op jit(solution)/shard_map/ppermute | solution.py:29
  20.2 5.8 %collective-permute-start.11 = (f32[2,18,1,256]{3,2,1,0:T(1,128)S(1)}, f32[2,18,1,256]{3,2,1,0:T(1,128)S(1)}, u32[]{:S(2)}, u32[]{:S(2)}) collective-permute-start(f32[2,18,1,256]{3,2,1,0:T(1,128)S(1)} %get-tuple-element.149), channel_id=1, source_target_pairs={{0,1},{1,2},{2,3},{3,0},{4,5},{5,6},{6,7},{7,4},{8,9},{9,10},{10,1... | collective-permute-start | bytes 110600 | tf_op jit(solution)/shard_map/ppermute | solution.py:26
  30.9 249.9 %reduce-scatter.5.cloned.1.call-start = ((), (), s32[]{:S(2)}) async-start(), calls=%async_computation.4 | async-start | bytes 5242880 | tf_op jit(solution)/shard_map/reduce_scatter | solution.py:87
  106.1 5.9 %collective-permute-start.14 = (f32[2,18,1,256]{3,2,1,0:T(1,128)S(1)}, f32[2,18,1,256]{3,2,1,0:T(1,128)S(1)}, u32[]{:S(2)}, u32[]{:S(2)}) collective-permute-start(f32[2,18,1,256]{3,2,1,0:T(1,128)S(1)} %get-tuple-element.146), channel_id=1, source_target_pairs={{0,1},{1,2},{2,3},{3,0},{4,5},{5,6},{6,7},{7,4},{8,9},{9,10},{10,1... | collective-permute-start | bytes 110600 | tf_op jit(solution)/shard_map/ppermute | solution.py:26
  114.3 5.6 %collective-permute-start.1 = (f32[2,2,32,256]{3,2,1,0:T(8,128)S(1)}, f32[2,2,32,256]{3,2,1,0:T(8,128)S(1)}, u32[]{:S(2)}, u32[]{:S(2)}) collective-permute-start(f32[2,2,32,256]{3,2,1,0:T(8,128)S(1)} %get-tuple-element.254), channel_id=1, source_target_pairs={{4,0},{0,4},{5,1},{1,5},{6,2},{2,6},{7,3},{3,7},{12,8},{8,12},{13,... | collective-permute-start | bytes 393224 | tf_op jit(solution)/shard_map/while/body/eval_jaxpr/ppermute | solution.py:29
  119.9 6.4 %collective-permute-start.2 = (f32[2,20,2,256]{3,2,1,0:T(2,128)S(1)}, f32[2,20,2,256]{3,2,1,0:T(2,128)S(1)}, u32[]{:S(2)}, u32[]{:S(2)}) collective-permute-start(f32[2,20,2,256]{3,2,1,0:T(2,128)S(1)} %get-tuple-element.255), channel_id=1, source_target_pairs={{0,1},{1,2},{2,3},{3,0},{4,5},{5,6},{6,7},{7,4},{8,9},{9,10},{10,1... | collective-permute-start | bytes 245768 | tf_op jit(solution)/shard_map/while/body/eval_jaxpr/ppermute | solution.py:26
  121.0 5.3 %collective-permute-start.3 = (f32[2,20,2,256]{3,2,1,0:T(2,128)S(1)}, f32[2,20,2,256]{3,2,1,0:T(2,128)S(1)}, u32[]{:S(2)}, u32[]{:S(2)}) collective-permute-start(f32[2,20,2,256]{3,2,1,0:T(2,128)S(1)} %get-tuple-element.256), channel_id=1, source_target_pairs={{1,0},{2,1},{3,2},{0,3},{5,4},{6,5},{7,6},{4,7},{9,8},{10,9},{11,1... | collective-permute-start | bytes 245768 | tf_op jit(solution)/shard_map/while/body/eval_jaxpr/ppermute | solution.py:29
  131.6 5.6 %collective-permute-start.1 = (f32[2,2,32,256]{3,2,1,0:T(8,128)S(1)}, f32[2,2,32,256]{3,2,1,0:T(8,128)S(1)}, u32[]{:S(2)}, u32[]{:S(2)}) collective-permute-start(f32[2,2,32,256]{3,2,1,0:T(8,128)S(1)} %get-tuple-element.254), channel_id=1, source_target_pairs={{4,0},{0,4},{5,1},{1,5},{6,2},{2,6},{7,3},{3,7},{12,8},{8,12},{13,... | collective-permute-start | bytes 393224 | tf_op jit(solution)/shard_map/while/body/eval_jaxpr/ppermute | solution.py:29
  137.3 6.4 %collective-permute-start.2 = (f32[2,20,2,256]{3,2,1,0:T(2,128)S(1)}, f32[2,20,2,256]{3,2,1,0:T(2,128)S(1)}, u32[]{:S(2)}, u32[]{:S(2)}) collective-permute-start(f32[2,20,2,256]{3,2,1,0:T(2,128)S(1)} %get-tuple-element.255), channel_id=1, source_target_pairs={{0,1},{1,2},{2,3},{3,0},{4,5},{5,6},{6,7},{7,4},{8,9},{9,10},{10,1... | collective-permute-start | bytes 245768 | tf_op jit(solution)/shard_map/while/body/eval_jaxpr/ppermute | solution.py:26
  138.6 5.3 %collective-permute-start.3 = (f32[2,20,2,256]{3,2,1,0:T(2,128)S(1)}, f32[2,20,2,256]{3,2,1,0:T(2,128)S(1)}, u32[]{:S(2)}, u32[]{:S(2)}) collective-permute-start(f32[2,20,2,256]{3,2,1,0:T(2,128)S(1)} %get-tuple-element.256), channel_id=1, source_target_pairs={{1,0},{2,1},{3,2},{0,3},{5,4},{6,5},{7,6},{4,7},{9,8},{10,9},{11,1... | collective-permute-start | bytes 245768 | tf_op jit(solution)/shard_map/while/body/eval_jaxpr/ppermute | solution.py:29
  149.2 5.6 %collective-permute-start.1 = (f32[2,2,32,256]{3,2,1,0:T(8,128)S(1)}, f32[2,2,32,256]{3,2,1,0:T(8,128)S(1)}, u32[]{:S(2)}, u32[]{:S(2)}) collective-permute-start(f32[2,2,32,256]{3,2,1,0:T(8,128)S(1)} %get-tuple-element.254), channel_id=1, source_target_pairs={{4,0},{0,4},{5,1},{1,5},{6,2},{2,6},{7,3},{3,7},{12,8},{8,12},{13,... | collective-permute-start | bytes 393224 | tf_op jit(solution)/shard_map/while/body/eval_jaxpr/ppermute | solution.py:29
  154.8 6.4 %collective-permute-start.2 = (f32[2,20,2,256]{3,2,1,0:T(2,128)S(1)}, f32[2,20,2,256]{3,2,1,0:T(2,128)S(1)}, u32[]{:S(2)}, u32[]{:S(2)}) collective-permute-start(f32[2,20,2,256]{3,2,1,0:T(2,128)S(1)} %get-tuple-element.255), channel_id=1, source_target_pairs={{0,1},{1,2},{2,3},{3,0},{4,5},{5,6},{6,7},{7,4},{8,9},{9,10},{10,1... | collective-permute-start | bytes 245768 | tf_op jit(solution)/shard_map/while/body/eval_jaxpr/ppermute | solution.py:26
  156.0 5.3 %collective-permute-start.3 = (f32[2,20,2,256]{3,2,1,0:T(2,128)S(1)}, f32[2,20,2,256]{3,2,1,0:T(2,128)S(1)}, u32[]{:S(2)}, u32[]{:S(2)}) collective-permute-start(f32[2,20,2,256]{3,2,1,0:T(2,128)S(1)} %get-tuple-element.256), channel_id=1, source_target_pairs={{1,0},{2,1},{3,2},{0,3},{5,4},{6,5},{7,6},{4,7},{9,8},{10,9},{11,1... | collective-permute-start | bytes 245768 | tf_op jit(solution)/shard_map/while/body/eval_jaxpr/ppermute | solution.py:29
  166.6 5.6 %collective-permute-start.1 = (f32[2,2,32,256]{3,2,1,0:T(8,128)S(1)}, f32[2,2,32,256]{3,2,1,0:T(8,128)S(1)}, u32[]{:S(2)}, u32[]{:S(2)}) collective-permute-start(f32[2,2,32,256]{3,2,1,0:T(8,128)S(1)} %get-tuple-element.254), channel_id=1, source_target_pairs={{4,0},{0,4},{5,1},{1,5},{6,2},{2,6},{7,3},{3,7},{12,8},{8,12},{13,... | collective-permute-start | bytes 393224 | tf_op jit(solution)/shard_map/while/body/eval_jaxpr/ppermute | solution.py:29
  172.2 6.4 %collective-permute-start.2 = (f32[2,20,2,256]{3,2,1,0:T(2,128)S(1)}, f32[2,20,2,256]{3,2,1,0:T(2,128)S(1)}, u32[]{:S(2)}, u32[]{:S(2)}) collective-permute-start(f32[2,20,2,256]{3,2,1,0:T(2,128)S(1)} %get-tuple-element.255), channel_id=1, source_target_pairs={{0,1},{1,2},{2,3},{3,0},{4,5},{5,6},{6,7},{7,4},{8,9},{9,10},{10,1... | collective-permute-start | bytes 245768 | tf_op jit(solution)/shard_map/while/body/eval_jaxpr/ppermute | solution.py:26
  173.5 5.3 %collective-permute-start.3 = (f32[2,20,2,256]{3,2,1,0:T(2,128)S(1)}, f32[2,20,2,256]{3,2,1,0:T(2,128)S(1)}, u32[]{:S(2)}, u32[]{:S(2)}) collective-permute-start(f32[2,20,2,256]{3,2,1,0:T(2,128)S(1)} %get-tuple-element.256), channel_id=1, source_target_pairs={{1,0},{2,1},{3,2},{0,3},{5,4},{6,5},{7,6},{4,7},{9,8},{10,9},{11,1... | collective-permute-start | bytes 245768 | tf_op jit(solution)/shard_map/while/body/eval_jaxpr/ppermute | solution.py:29
  184.1 5.6 %collective-permute-start.1 = (f32[2,2,32,256]{3,2,1,0:T(8,128)S(1)}, f32[2,2,32,256]{3,2,1,0:T(8,128)S(1)}, u32[]{:S(2)}, u32[]{:S(2)}) collective-permute-start(f32[2,2,32,256]{3,2,1,0:T(8,128)S(1)} %get-tuple-element.254), channel_id=1, source_target_pairs={{4,0},{0,4},{5,1},{1,5},{6,2},{2,6},{7,3},{3,7},{12,8},{8,12},{13,... | collective-permute-start | bytes 393224 | tf_op jit(solution)/shard_map/while/body/eval_jaxpr/ppermute | solution.py:29
  189.8 6.4 %collective-permute-start.2 = (f32[2,20,2,256]{3,2,1,0:T(2,128)S(1)}, f32[2,20,2,256]{3,2,1,0:T(2,128)S(1)}, u32[]{:S(2)}, u32[]{:S(2)}) collective-permute-start(f32[2,20,2,256]{3,2,1,0:T(2,128)S(1)} %get-tuple-element.255), channel_id=1, source_target_pairs={{0,1},{1,2},{2,3},{3,0},{4,5},{5,6},{6,7},{7,4},{8,9},{9,10},{10,1... | collective-permute-start | bytes 245768 | tf_op jit(solution)/shard_map/while/body/eval_jaxpr/ppermute | solution.py:26
  190.9 5.4 %collective-permute-start.3 = (f32[2,20,2,256]{3,2,1,0:T(2,128)S(1)}, f32[2,20,2,256]{3,2,1,0:T(2,128)S(1)}, u32[]{:S(2)}, u32[]{:S(2)}) collective-permute-start(f32[2,20,2,256]{3,2,1,0:T(2,128)S(1)} %get-tuple-element.256), channel_id=1, source_target_pairs={{1,0},{2,1},{3,2},{0,3},{5,4},{6,5},{7,6},{4,7},{9,8},{10,9},{11,1... | collective-permute-start | bytes 245768 | tf_op jit(solution)/shard_map/while/body/eval_jaxpr/ppermute | solution.py:29
  201.7 6.6 %collective-permute-start.1 = (f32[2,2,32,256]{3,2,1,0:T(8,128)S(1)}, f32[2,2,32,256]{3,2,1,0:T(8,128)S(1)}, u32[]{:S(2)}, u32[]{:S(2)}) collective-permute-start(f32[2,2,32,256]{3,2,1,0:T(8,128)S(1)} %get-tuple-element.254), channel_id=1, source_target_pairs={{4,0},{0,4},{5,1},{1,5},{6,2},{2,6},{7,3},{3,7},{12,8},{8,12},{13,... | collective-permute-start | bytes 393224 | tf_op jit(solution)/shard_map/while/body/eval_jaxpr/ppermute | solution.py:29
  208.4 6.5 %collective-permute-start.2 = (f32[2,20,2,256]{3,2,1,0:T(2,128)S(1)}, f32[2,20,2,256]{3,2,1,0:T(2,128)S(1)}, u32[]{:S(2)}, u32[]{:S(2)}) collective-permute-start(f32[2,20,2,256]{3,2,1,0:T(2,128)S(1)} %get-tuple-element.255), channel_id=1, source_target_pairs={{0,1},{1,2},{2,3},{3,0},{4,5},{5,6},{6,7},{7,4},{8,9},{9,10},{10,1... | collective-permute-start | bytes 245768 | tf_op jit(solution)/shard_map/while/body/eval_jaxpr/ppermute | solution.py:26
  209.9 5.3 %collective-permute-start.3 = (f32[2,20,2,256]{3,2,1,0:T(2,128)S(1)}, f32[2,20,2,256]{3,2,1,0:T(2,128)S(1)}, u32[]{:S(2)}, u32[]{:S(2)}) collective-permute-start(f32[2,20,2,256]{3,2,1,0:T(2,128)S(1)} %get-tuple-element.256), channel_id=1, source_target_pairs={{1,0},{2,1},{3,2},{0,3},{5,4},{6,5},{7,6},{4,7},{9,8},{10,9},{11,1... | collective-permute-start | bytes 245768 | tf_op jit(solution)/shard_map/while/body/eval_jaxpr/ppermute | solution.py:29
  220.0 5.3 %collective-permute-start.16 = (f32[2,1,32,256]{3,2,1,0:T(8,128)S(1)}, f32[2,1,32,256]{3,2,1,0:T(8,128)S(1)}, u32[]{:S(2)}, u32[]{:S(2)}) collective-permute-start(f32[2,1,32,256]{3,2,1,0:T(8,128)S(1)} %get-tuple-element.152), channel_id=1, source_target_pairs={{4,0},{0,4},{5,1},{1,5},{6,2},{2,6},{7,3},{3,7},{12,8},{8,12},{13,... | collective-permute-start | bytes 196616 | tf_op jit(solution)/shard_map/ppermute | solution.py:29
  225.4 5.1 %collective-permute-start.18 = (f32[2,18,1,256]{3,2,1,0:T(1,128)S(1)}, f32[2,18,1,256]{3,2,1,0:T(1,128)S(1)}, u32[]{:S(2)}, u32[]{:S(2)}) collective-permute-start(f32[2,18,1,256]{3,2,1,0:T(1,128)S(1)} %get-tuple-element.144), channel_id=1, source_target_pairs={{1,0},{2,1},{3,2},{0,3},{5,4},{6,5},{7,6},{4,7},{9,8},{10,9},{11,1... | collective-permute-start | bytes 110600 | tf_op jit(solution)/shard_map/ppermute | solution.py:29
  228.8 5.8 %collective-permute-start.19 = (f32[2,18,1,256]{3,2,1,0:T(1,128)S(1)}, f32[2,18,1,256]{3,2,1,0:T(1,128)S(1)}, u32[]{:S(2)}, u32[]{:S(2)}) collective-permute-start(f32[2,18,1,256]{3,2,1,0:T(1,128)S(1)} %get-tuple-element.145), channel_id=1, source_target_pairs={{0,1},{1,2},{2,3},{3,0},{4,5},{5,6},{6,7},{7,4},{8,9},{9,10},{10,1... | collective-permute-start | bytes 110600 | tf_op jit(solution)/shard_map/ppermute | solution.py:26
  289.2 5.9 %collective-permute-start.22 = (f32[2,18,1,256]{3,2,1,0:T(1,128)S(1)}, f32[2,18,1,256]{3,2,1,0:T(1,128)S(1)}, u32[]{:S(2)}, u32[]{:S(2)}) collective-permute-start(f32[2,18,1,256]{3,2,1,0:T(1,128)S(1)} %get-tuple-element.142), channel_id=1, source_target_pairs={{0,1},{1,2},{2,3},{3,0},{4,5},{5,6},{6,7},{7,4},{8,9},{9,10},{10,1... | collective-permute-start | bytes 110600 | tf_op jit(solution)/shard_map/ppermute | solution.py:26
  297.3 5.6 %collective-permute-start.5 = (f32[2,2,32,256]{3,2,1,0:T(8,128)S(1)}, f32[2,2,32,256]{3,2,1,0:T(8,128)S(1)}, u32[]{:S(2)}, u32[]{:S(2)}) collective-permute-start(f32[2,2,32,256]{3,2,1,0:T(8,128)S(1)} %get-tuple-element.273), channel_id=1, source_target_pairs={{4,0},{0,4},{5,1},{1,5},{6,2},{2,6},{7,3},{3,7},{12,8},{8,12},{13,... | collective-permute-start | bytes 393224 | tf_op jit(solution)/shard_map/while/body/eval_jaxpr/ppermute | solution.py:29
  303.0 6.4 %collective-permute-start.6 = (f32[2,20,2,256]{3,2,1,0:T(2,128)S(1)}, f32[2,20,2,256]{3,2,1,0:T(2,128)S(1)}, u32[]{:S(2)}, u32[]{:S(2)}) collective-permute-start(f32[2,20,2,256]{3,2,1,0:T(2,128)S(1)} %get-tuple-element.274), channel_id=1, source_target_pairs={{0,1},{1,2},{2,3},{3,0},{4,5},{5,6},{6,7},{7,4},{8,9},{9,10},{10,1... | collective-permute-start | bytes 245768 | tf_op jit(solution)/shard_map/while/body/eval_jaxpr/ppermute | solution.py:26
  304.1 5.3 %collective-permute-start.7 = (f32[2,20,2,256]{3,2,1,0:T(2,128)S(1)}, f32[2,20,2,256]{3,2,1,0:T(2,128)S(1)}, u32[]{:S(2)}, u32[]{:S(2)}) collective-permute-start(f32[2,20,2,256]{3,2,1,0:T(2,128)S(1)} %get-tuple-element.275), channel_id=1, source_target_pairs={{1,0},{2,1},{3,2},{0,3},{5,4},{6,5},{7,6},{4,7},{9,8},{10,9},{11,1... | collective-permute-start | bytes 245768 | tf_op jit(solution)/shard_map/while/body/eval_jaxpr/ppermute | solution.py:29
  314.7 5.6 %collective-permute-start.5 = (f32[2,2,32,256]{3,2,1,0:T(8,128)S(1)}, f32[2,2,32,256]{3,2,1,0:T(8,128)S(1)}, u32[]{:S(2)}, u32[]{:S(2)}) collective-permute-start(f32[2,2,32,256]{3,2,1,0:T(8,128)S(1)} %get-tuple-element.273), channel_id=1, source_target_pairs={{4,0},{0,4},{5,1},{1,5},{6,2},{2,6},{7,3},{3,7},{12,8},{8,12},{13,... | collective-permute-start | bytes 393224 | tf_op jit(solution)/shard_map/while/body/eval_jaxpr/ppermute | solution.py:29
  320.3 6.4 %collective-permute-start.6 = (f32[2,20,2,256]{3,2,1,0:T(2,128)S(1)}, f32[2,20,2,256]{3,2,1,0:T(2,128)S(1)}, u32[]{:S(2)}, u32[]{:S(2)}) collective-permute-start(f32[2,20,2,256]{3,2,1,0:T(2,128)S(1)} %get-tuple-element.274), channel_id=1, source_target_pairs={{0,1},{1,2},{2,3},{3,0},{4,5},{5,6},{6,7},{7,4},{8,9},{9,10},{10,1... | collective-permute-start | bytes 245768 | tf_op jit(solution)/shard_map/while/body/eval_jaxpr/ppermute | solution.py:26
  321.7 5.3 %collective-permute-start.7 = (f32[2,20,2,256]{3,2,1,0:T(2,128)S(1)}, f32[2,20,2,256]{3,2,1,0:T(2,128)S(1)}, u32[]{:S(2)}, u32[]{:S(2)}) collective-permute-start(f32[2,20,2,256]{3,2,1,0:T(2,128)S(1)} %get-tuple-element.275), channel_id=1, source_target_pairs={{1,0},{2,1},{3,2},{0,3},{5,4},{6,5},{7,6},{4,7},{9,8},{10,9},{11,1... | collective-permute-start | bytes 245768 | tf_op jit(solution)/shard_map/while/body/eval_jaxpr/ppermute | solution.py:29
  332.2 5.6 %collective-permute-start.5 = (f32[2,2,32,256]{3,2,1,0:T(8,128)S(1)}, f32[2,2,32,256]{3,2,1,0:T(8,128)S(1)}, u32[]{:S(2)}, u32[]{:S(2)}) collective-permute-start(f32[2,2,32,256]{3,2,1,0:T(8,128)S(1)} %get-tuple-element.273), channel_id=1, source_target_pairs={{4,0},{0,4},{5,1},{1,5},{6,2},{2,6},{7,3},{3,7},{12,8},{8,12},{13,... | collective-permute-start | bytes 393224 | tf_op jit(solution)/shard_map/while/body/eval_jaxpr/ppermute | solution.py:29
  337.9 6.4 %collective-permute-start.6 = (f32[2,20,2,256]{3,2,1,0:T(2,128)S(1)}, f32[2,20,2,256]{3,2,1,0:T(2,128)S(1)}, u32[]{:S(2)}, u32[]{:S(2)}) collective-permute-start(f32[2,20,2,256]{3,2,1,0:T(2,128)S(1)} %get-tuple-element.274), channel_id=1, source_target_pairs={{0,1},{1,2},{2,3},{3,0},{4,5},{5,6},{6,7},{7,4},{8,9},{9,10},{10,1... | collective-permute-start | bytes 245768 | tf_op jit(solution)/shard_map/while/body/eval_jaxpr/ppermute | solution.py:26
  339.0 5.3 %collective-permute-start.7 = (f32[2,20,2,256]{3,2,1,0:T(2,128)S(1)}, f32[2,20,2,256]{3,2,1,0:T(2,128)S(1)}, u32[]{:S(2)}, u32[]{:S(2)}) collective-permute-start(f32[2,20,2,256]{3,2,1,0:T(2,128)S(1)} %get-tuple-element.275), channel_id=1, source_target_pairs={{1,0},{2,1},{3,2},{0,3},{5,4},{6,5},{7,6},{4,7},{9,8},{10,9},{11,1... | collective-permute-start | bytes 245768 | tf_op jit(solution)/shard_map/while/body/eval_jaxpr/ppermute | solution.py:29
  349.6 5.6 %collective-permute-start.5 = (f32[2,2,32,256]{3,2,1,0:T(8,128)S(1)}, f32[2,2,32,256]{3,2,1,0:T(8,128)S(1)}, u32[]{:S(2)}, u32[]{:S(2)}) collective-permute-start(f32[2,2,32,256]{3,2,1,0:T(8,128)S(1)} %get-tuple-element.273), channel_id=1, source_target_pairs={{4,0},{0,4},{5,1},{1,5},{6,2},{2,6},{7,3},{3,7},{12,8},{8,12},{13,... | collective-permute-start | bytes 393224 | tf_op jit(solution)/shard_map/while/body/eval_jaxpr/ppermute | solution.py:29
  355.3 6.4 %collective-permute-start.6 = (f32[2,20,2,256]{3,2,1,0:T(2,128)S(1)}, f32[2,20,2,256]{3,2,1,0:T(2,128)S(1)}, u32[]{:S(2)}, u32[]{:S(2)}) collective-permute-start(f32[2,20,2,256]{3,2,1,0:T(2,128)S(1)} %get-tuple-element.274), channel_id=1, source_target_pairs={{0,1},{1,2},{2,3},{3,0},{4,5},{5,6},{6,7},{7,4},{8,9},{9,10},{10,1... | collective-permute-start | bytes 245768 | tf_op jit(solution)/shard_map/while/body/eval_jaxpr/ppermute | solution.py:26
  356.6 5.3 %collective-permute-start.7 = (f32[2,20,2,256]{3,2,1,0:T(2,128)S(1)}, f32[2,20,2,256]{3,2,1,0:T(2,128)S(1)}, u32[]{:S(2)}, u32[]{:S(2)}) collective-permute-start(f32[2,20,2,256]{3,2,1,0:T(2,128)S(1)} %get-tuple-element.275), channel_id=1, source_target_pairs={{1,0},{2,1},{3,2},{0,3},{5,4},{6,5},{7,6},{4,7},{9,8},{10,9},{11,1... | collective-permute-start | bytes 245768 | tf_op jit(solution)/shard_map/while/body/eval_jaxpr/ppermute | solution.py:29
  367.2 5.6 %collective-permute-start.5 = (f32[2,2,32,256]{3,2,1,0:T(8,128)S(1)}, f32[2,2,32,256]{3,2,1,0:T(8,128)S(1)}, u32[]{:S(2)}, u32[]{:S(2)}) collective-permute-start(f32[2,2,32,256]{3,2,1,0:T(8,128)S(1)} %get-tuple-element.273), channel_id=1, source_target_pairs={{4,0},{0,4},{5,1},{1,5},{6,2},{2,6},{7,3},{3,7},{12,8},{8,12},{13,... | collective-permute-start | bytes 393224 | tf_op jit(solution)/shard_map/while/body/eval_jaxpr/ppermute | solution.py:29
  372.8 6.4 %collective-permute-start.6 = (f32[2,20,2,256]{3,2,1,0:T(2,128)S(1)}, f32[2,20,2,256]{3,2,1,0:T(2,128)S(1)}, u32[]{:S(2)}, u32[]{:S(2)}) collective-permute-start(f32[2,20,2,256]{3,2,1,0:T(2,128)S(1)} %get-tuple-element.274), channel_id=1, source_target_pairs={{0,1},{1,2},{2,3},{3,0},{4,5},{5,6},{6,7},{7,4},{8,9},{9,10},{10,1... | collective-permute-start | bytes 245768 | tf_op jit(solution)/shard_map/while/body/eval_jaxpr/ppermute | solution.py:26
  374.0 5.4 %collective-permute-start.7 = (f32[2,20,2,256]{3,2,1,0:T(2,128)S(1)}, f32[2,20,2,256]{3,2,1,0:T(2,128)S(1)}, u32[]{:S(2)}, u32[]{:S(2)}) collective-permute-start(f32[2,20,2,256]{3,2,1,0:T(2,128)S(1)} %get-tuple-element.275), channel_id=1, source_target_pairs={{1,0},{2,1},{3,2},{0,3},{5,4},{6,5},{7,6},{4,7},{9,8},{10,9},{11,1... | collective-permute-start | bytes 245768 | tf_op jit(solution)/shard_map/while/body/eval_jaxpr/ppermute | solution.py:29
  384.7 5.5 %collective-permute-start.5 = (f32[2,2,32,256]{3,2,1,0:T(8,128)S(1)}, f32[2,2,32,256]{3,2,1,0:T(8,128)S(1)}, u32[]{:S(2)}, u32[]{:S(2)}) collective-permute-start(f32[2,2,32,256]{3,2,1,0:T(8,128)S(1)} %get-tuple-element.273), channel_id=1, source_target_pairs={{4,0},{0,4},{5,1},{1,5},{6,2},{2,6},{7,3},{3,7},{12,8},{8,12},{13,... | collective-permute-start | bytes 393224 | tf_op jit(solution)/shard_map/while/body/eval_jaxpr/ppermute | solution.py:29
  390.3 6.4 %collective-permute-start.6 = (f32[2,20,2,256]{3,2,1,0:T(2,128)S(1)}, f32[2,20,2,256]{3,2,1,0:T(2,128)S(1)}, u32[]{:S(2)}, u32[]{:S(2)}) collective-permute-start(f32[2,20,2,256]{3,2,1,0:T(2,128)S(1)} %get-tuple-element.274), channel_id=1, source_target_pairs={{0,1},{1,2},{2,3},{3,0},{4,5},{5,6},{6,7},{7,4},{8,9},{9,10},{10,1... | collective-permute-start | bytes 245768 | tf_op jit(solution)/shard_map/while/body/eval_jaxpr/ppermute | solution.py:26
  391.5 5.3 %collective-permute-start.7 = (f32[2,20,2,256]{3,2,1,0:T(2,128)S(1)}, f32[2,20,2,256]{3,2,1,0:T(2,128)S(1)}, u32[]{:S(2)}, u32[]{:S(2)}) collective-permute-start(f32[2,20,2,256]{3,2,1,0:T(2,128)S(1)} %get-tuple-element.275), channel_id=1, source_target_pairs={{1,0},{2,1},{3,2},{0,3},{5,4},{6,5},{7,6},{4,7},{9,8},{10,9},{11,1... | collective-permute-start | bytes 245768 | tf_op jit(solution)/shard_map/while/body/eval_jaxpr/ppermute | solution.py:29
  (41 other events, 190.4 us)
Sparse Core Ops, SparseCore 0:
  12.1 37.9 all-reduce.1
  52.7 45.0 reduce-scatter.2
  239.2 41.5 reduce-scatter.4
where the time goes:
time: 409 us
  waiting for transfers between devices  216 us (53%)
  starting transfers between devices  96.6 us (24%)
  other arithmetic  44.3 us (11%)
  local copies, waits for them, and re-layouts  36.9 us (9%)
  between operations  13.9 us (3%)
    reduce_scatter x2, waiting for transfers between devices, body(): lax.psum_scatter(section_terms, 'node', scatter_dimension=0, tiled=True)[0]  89.3 us
    ppermute x32, waiting for transfers between devices, padded_2(): lax.ppermute(lax.slice_in_dim(block, block.shape[dim] - width, None, axis...  85.6 us
    ppermute x32, starting transfers between devices, padded_2(): lax.ppermute(lax.slice_in_dim(block, 0, width, axis=dim), axis, backward)  60.6 us
    ppermute x32, starting transfers between devices, padded_2(): lax.ppermute(lax.slice_in_dim(block, block.shape[dim] - width, None, axis...  35.9 us
    ppermute x32, waiting for transfers between devices, padded_2(): lax.ppermute(lax.slice_in_dim(block, 0, width, axis=dim), axis, backward)  23 us
    slice x52, local copies, waits for them, and re-layouts, beside(): return total + jnp.roll(center, 1, 3) + jnp.roll(center, -1, 3)  20.7 us
    psum x1, waiting for transfers between devices, from_root(): return lax.psum(kept, axis)  18 us
    div x12, other arithmetic, double_turn(): midway = (extended + coef * beside(beside_all)) / (1.0 + 6.0 * coef)  12.1 us
  transfers between devices with their start and end apart: 67, of which 62 were waited for; matrix products, arithmetic and copies ran while one was open for 3% of the time, Pallas kernels for 0%

commit v1 on v0

--- a/solution.py
+++ b/solution.py
@@ -1,7 +1,13 @@
 import jax
 import jax.numpy as jnp
 from jax import lax
+from jax.experimental import pallas as pl
+from jax.experimental.pallas import tpu as pltpu
 from jax.sharding import PartitionSpec as P
+
+MESH = pl.DeviceIdType.MESH
+WIDTH = 4
+CHUNKS = 4
 
 SWEEPS = 2
 JACOBI = 12
@@ -97,9 +103,301 @@
     return iterate[None]
 
 
+def pick(values, index):
+    out = jnp.float32(values[-1])
+    for at in range(len(values) - 1):
+        out = jnp.where(index == at, jnp.float32(values[at]), out)
+    return out
+
+
+def pick_pair(table, row, column):
+    out = pick(table[-1], column)
+    for at in range(len(table) - 1):
+        out = jnp.where(row == at, pick(table[at], column), out)
+    return out
+
+
+def kernel(
+    sy_count, x_ref, f_ref, k_ref, out_ref,
+    xe, edge_out, edge_in, diff, force, force_in, start, part_out, part_in,
+    local, right_out, rj, xj, halo_out, halo_in, back, send_sems, recv_sems,
+):
+    w = WIDTH
+    _, ny, nx, nz = x_ref.shape
+    full = 2 * nx
+    step = ny // CHUNKS
+    m, s, t = lax.axis_index("node"), lax.axis_index("sx"), lax.axis_index("sy")
+    other = 1 - s
+    core = {"node": m + 1 - 2 * lax.rem(m, 2)}
+    across = {"node": lax.rem(m + 2, 4)}
+    pair = {"sx": other}
+    up = {"sy": lax.rem(t + 1, sy_count)}
+    down = {"sy": lax.rem(t + sy_count - 1, sy_count)}
+    m1, m2 = core["node"], across["node"]
+    count = [0]
+
+    def send(src, dst, target):
+        at = count[0]
+        count[0] += 1
+        copy = pltpu.make_async_remote_copy(
+            src_ref=src, dst_ref=dst, send_sem=send_sems.at[at], recv_sem=recv_sems.at[at],
+            device_id=target, device_id_type=MESH,
+        )
+        copy.start()
+        started.append(copy)
+        return copy
+
+    started = []
+    barrier = pltpu.get_barrier_semaphore()
+    for target in (core, across, pair, up, down):
+        pl.semaphore_signal(barrier, inc=1, device_id=target, device_id_type=MESH)
+
+    table = collocation()
+    h = time_step
+    q_own, q_core = h * pick_pair(table, m, m), h * pick_pair(table, m, m1)
+    p_own, p_core = h * pick_pair(table, m2, m), h * pick_pair(table, m2, m1)
+    tau = pick(radau_points, m)
+    has_start = jnp.where(m >= 2, jnp.float32(1.0), jnp.float32(0.0))
+    scale = [1.0 / (1.0 + 6.0 * h * tau * d) for d in diffusion_values]
+    coef_s = h * tau * pick(diffusion_values, s)
+    gain = coef_s / (1.0 + 6.0 * coef_s)
+    own_rows = pl.ds(pl.multiple_of(nx * s, nx), nx)
+    other_rows = pl.ds(pl.multiple_of(nx * other, nx), nx)
+    row = lax.broadcasted_iota(jnp.int32, (nx, nz), 0)
+
+    def planes(first, last, fn, unroll=1):
+        def go(y, carry):
+            fn(y)
+            return carry
+        if last > first:
+            lax.fori_loop(first, last, go, 0, unroll=unroll)
+
+    def load(y):
+        for a in range(2):
+            xe[0, a, y + 1] = x_ref[a, y]
+        xj[0, y + w, own_rows, :] = x_ref[s, y]
+
+    planes(0, ny, load)
+    pl.semaphore_wait(barrier, 5)
+
+    exchanges = 0
+    first_pair = None
+    for sweep in range(SWEEPS):
+        x = xe.at[sweep]
+
+        def edges(y):
+            for a in range(2):
+                edge_out[sweep, 0, a, pl.ds(y, 1), :] = x[a, y + 1, pl.ds(0, 1), :]
+                edge_out[sweep, 1, a, pl.ds(y, 1), :] = x[a, y + 1, pl.ds(nx - 1, 1), :]
+
+        edge_copies = [
+            send(x.at[:, ny], x.at[:, 0], up),
+            send(x.at[:, 1], x.at[:, ny + 1], down),
+        ]
+        planes(0, ny, edges)
+        edge_copies += [
+            send(edge_out.at[sweep, 1], edge_in.at[sweep, 0], pair),
+            send(edge_out.at[sweep, 0], edge_in.at[sweep, 1], pair),
+        ]
+        start_copy = None
+        if sweep == 0:
+            start_copy = send(x_ref, start, core)
+            first_pair = send(x_ref.at[other], xj.at[0, pl.ds(w, ny), own_rows, :], pair)
+        for copy in edge_copies:
+            copy.wait_recv()
+
+        def forces(y):
+            u, v = x[0, y + 1], x[1, y + 1]
+            feed, kill = f_ref[y], k_ref[y]
+            uvv = u * v * v
+            react = (feed * (1.0 - u) - uvv, uvv - (feed + kill) * v)
+            for a, value in enumerate((u, v)):
+                low = edge_in[sweep, 0, a, pl.ds(y, 1), :]
+                high = edge_in[sweep, 1, a, pl.ds(y, 1), :]
+                total = x[a, y] + x[a, y + 2]
+                total = total + jnp.where(row == 0, low, pltpu.roll(value, 1, 0))
+                total = total + jnp.where(row == nx - 1, high, pltpu.roll(value, nx - 1, 0))
+                total = total + pltpu.roll(value, 1, 1) + pltpu.roll(value, nz - 1, 1)
+                d = diffusion_values[a] * (total - 6.0 * value)
+                diff[a, y] = d
+                force[sweep, a, y] = d + react[a]
+
+        order = [0, CHUNKS - 1] + list(range(1, CHUNKS - 1))
+        core_copies, part_copies, right_copies = {}, {}, {}
+        for c in order:
+            rows = pl.ds(c * step, step)
+            planes(c * step, (c + 1) * step, forces)
+            core_copies[c] = send(
+                force.at[sweep, :, rows], force_in.at[sweep, :, rows], core
+            )
+        if sweep == 0:
+            start_copy.wait_recv()
+
+            def begin(y):
+                for a in range(2):
+                    first = jnp.where(lax.rem(m, 2) == 1, x_ref[a, y], start[a, y])
+                    start_kept[a, y] = has_start * first
+
+            start_kept = local.at[1]
+            planes(0, ny, begin)
+        start_kept = local.at[1]
+
+        def parts(y):
+            for a in range(2):
+                f, g, begin_value = force[sweep, a, y], force_in[sweep, a, y], start_kept[a, y]
+                part_out[sweep, a, y] = begin_value + p_own * f + p_core * g
+                local[0, a, y] = begin_value + q_own * f + q_core * g - (h * tau) * diff[a, y]
+
+        for c in order:
+            rows = pl.ds(c * step, step)
+            core_copies[c].wait_recv()
+            planes(c * step, (c + 1) * step, parts)
+            part_copies[c] = send(
+                part_out.at[sweep, :, rows], part_in.at[sweep, :, rows], across
+            )
+
+        scale_own = jnp.where(s == 0, scale[0], scale[1])
+        scale_other = jnp.where(s == 0, scale[1], scale[0])
+
+        def rights(y):
+            rj[sweep, y + w, own_rows, :] = (local[0, s, y] + part_in[sweep, s, y]) * scale_own
+            right_out[sweep, y] = (local[0, other, y] + part_in[sweep, other, y]) * scale_other
+
+        for c in order:
+            part_copies[c].wait_recv()
+            planes(c * step, (c + 1) * step, rights)
+            right_copies[c] = send(
+                right_out.at[sweep, pl.ds(c * step, step)],
+                rj.at[sweep, pl.ds(w + c * step, step), own_rows, :],
+                pair,
+            )
+        if sweep == 0:
+            first_pair.wait_recv()
+        for c in order[:2]:
+            right_copies[c].wait_recv()
+        right_halo = [
+            send(rj.at[sweep, pl.ds(w, w - 1)], rj.at[sweep, pl.ds(w + ny, w - 1)], down),
+            send(rj.at[sweep, pl.ds(w + ny - w + 1, w - 1)], rj.at[sweep, pl.ds(1, w - 1)], up),
+        ]
+        for block in range(JACOBI // w):
+            e = exchanges
+            exchanges += 1
+            for y in range(w):
+                halo_out[e, 0, y] = xj[0, w + y]
+                halo_out[e, 1, y] = xj[0, ny + y]
+            copies = [
+                send(halo_out.at[e, 0], halo_in.at[e, 0], down),
+                send(halo_out.at[e, 1], halo_in.at[e, 1], up),
+            ]
+            if block == 0:
+                for c in order[2:]:
+                    right_copies[c].wait_recv()
+
+            def sweep_planes(turn, first, last):
+                src, dst = (turn - 1) % 2, turn % 2
+
+                def one(y):
+                    value = xj[src, y]
+                    total = xj[src, y - 1] + xj[src, y + 1]
+                    total = total + pltpu.roll(value, 1, 0) + pltpu.roll(value, full - 1, 0)
+                    total = total + pltpu.roll(value, 1, 1) + pltpu.roll(value, nz - 1, 1)
+                    xj[dst, y] = rj[sweep, y] + gain * total
+
+                planes(first + w, last + w, one)
+
+            for turn in range(1, w + 1):
+                sweep_planes(turn, turn, ny - turn)
+            for copy in copies:
+                copy.wait_recv()
+            if block == 0:
+                for copy in right_halo:
+                    copy.wait_recv()
+            for y in range(w):
+                xj[0, w + ny + y] = halo_in[e, 0, y]
+                xj[0, y] = halo_in[e, 1, y]
+            for turn in range(1, w + 1):
+                sweep_planes(turn, turn - w, turn)
+                sweep_planes(turn, ny - turn, ny + w - turn)
+        source = xj.at[0, pl.ds(w, ny), other_rows, :]
+        if sweep < SWEEPS - 1:
+            copy = send(source, xe.at[sweep + 1, s, pl.ds(1, ny)], pair)
+
+            def keep(y):
+                xe[sweep + 1, s, y + 1] = xj[0, y + w, own_rows, :]
+
+            planes(0, ny, keep)
+            copy.wait_recv()
+            copy.wait_send()
+            started.pop()
+        else:
+            copy = send(source, back, pair)
+
+            def keep(y):
+                out_ref[s, y] = xj[0, y + w, own_rows, :]
+
+            planes(0, ny, keep)
+            copy.wait_recv()
+
+            def finish(y):
+                out_ref[other, y] = back[y]
+
+            planes(0, ny, finish)
+    for copy in started:
+        copy.wait_send()
+
+
+def fast_body(sy_count, previous, feed_rate, kill_rate):
+    f32 = jnp.float32
+    x = jnp.swapaxes(previous[0], 1, 2)
+    _, ny, nx, nz = x.shape
+    w = WIDTH
+    block = (2, ny, nx, nz)
+    blocks = SWEEPS * (JACOBI // w)
+    copies = SWEEPS * (4 + 3 * CHUNKS + 2 + 2 * (JACOBI // w) + 1) + 2
+    vmem = pl.BlockSpec(memory_space=pltpu.VMEM)
+    out = pl.pallas_call(
+        lambda *refs: kernel(sy_count, *refs),
+        out_shape=jax.ShapeDtypeStruct(block, f32),
+        in_specs=[vmem] * 3,
+        out_specs=vmem,
+        scratch_shapes=[
+            pltpu.VMEM((SWEEPS, 2, ny + 2, nx, nz), f32),
+            pltpu.VMEM((SWEEPS, 2, 2, ny, nz), f32),
+            pltpu.VMEM((SWEEPS, 2, 2, ny, nz), f32),
+            pltpu.VMEM(block, f32),
+            pltpu.VMEM((SWEEPS,) + block, f32),
+            pltpu.VMEM((SWEEPS,) + block, f32),
+            pltpu.VMEM(block, f32),
+            pltpu.VMEM((SWEEPS,) + block, f32),
+            pltpu.VMEM((SWEEPS,) + block, f32),
+            pltpu.VMEM((2,) + block, f32),
+            pltpu.VMEM((SWEEPS, ny, nx, nz), f32),
+            pltpu.VMEM((SWEEPS, ny + 2 * w, 2 * nx, nz), f32),
+            pltpu.VMEM((2, ny + 2 * w, 2 * nx, nz), f32),
+            pltpu.VMEM((blocks, 2, w, 2 * nx, nz), f32),
+            pltpu.VMEM((blocks, 2, w, 2 * nx, nz), f32),
+            pltpu.VMEM((ny, nx, nz), f32),
+            pltpu.SemaphoreType.DMA((copies,)),
+            pltpu.SemaphoreType.DMA((copies,)),
+        ],
+        compiler_params=pltpu.CompilerParams(
+            collective_id=0, has_side_effects=True, vmem_limit_bytes=48 * 1024 * 1024
+        ),
+    )(x, jnp.swapaxes(feed_rate, 0, 1), jnp.swapaxes(kill_rate, 0, 1))
+    return jnp.swapaxes(out, 1, 2)[None]
+
+
 def solution(mesh):
+    sizes = dict(mesh.shape)
+    fast = sizes["sx"] == 2 and sizes["node"] == len(radau_points) and sizes["sy"] > 2
+
+    def run(previous, feed_rate, kill_rate):
+        if fast:
+            return fast_body(sizes["sy"], previous, feed_rate, kill_rate)
+        return body(previous, feed_rate, kill_rate)
+
     return jax.shard_map(
-        body,
+        run,
         mesh=mesh,
         in_specs=(P("node", None, "sx", "sy", None), P("sx", "sy", None), P("sx", "sy", None)),
         out_specs=P("node", None, "sx", "sy", None),

time: 409 us -> 179 us (0.44)
  waiting for transfers between devices: 216 us -> 0 us
  Pallas kernels: 0 us -> 175 us
  starting transfers between devices: 96.6 us -> 0 us
  other arithmetic: 44.3 us -> 0 us
  local copies, waits for them, and re-layouts: 36.9 us -> 4.12 us
  between operations: 13.9 us -> 0.03 us
    pallas_call x0 -> x1, Pallas kernels: none -> 175 us  [fast_body(): pl.pallas_call(lambda *refs: kernel(sy_count, *refs), out_shape=jax.Shape...]
    ppermute x64 -> x0, waiting for transfers between devices: 109 us -> none  [the longest x32 85.6 us: padded_2(): lax.ppermute(lax.slice_in_dim(block, block.shape[dim] - width, None, axis...]
    ppermute x64 -> x0, starting transfers between devices: 96.5 us -> none  [the longest x32 60.6 us: padded_2(): lax.ppermute(lax.slice_in_dim(block, 0, width, axis=dim), axis, backward)]
    reduce_scatter x2 -> x0, waiting for transfers between devices: 89.3 us -> none  [body(): lax.psum_scatter(section_terms, 'node', scatter_dimension=0, tiled=True)[0]]
    div x24 -> x0, other arithmetic: 21.9 us -> none  [the longest x12 12.1 us: double_turn(): midway = (extended + coef * beside(beside_all)) / (1.0 + 6.0 * coef)]
    slice x81 -> x0, local copies, waits for them, and re-layouts: 21.7 us -> none  [the longest x52 20.7 us: beside(): return total + jnp.roll(center, 1, 3) + jnp.roll(center, -1, 3)]
    psum x1 -> x0, waiting for transfers between devices: 18 us -> none  [from_root(): return lax.psum(kept, axis)]
    while x48 -> x0, local copies, waits for them, and re-layouts: 10.8 us -> none
  transfers between devices with their start and end apart: 67 -> 0, of which waited for: 62 -> 0; matrix products, arithmetic and copies ran while one was open for 3% -> 0% of each run, Pallas kernels for 0% -> 0%
where the time goes in v1:
time: 179 us
  Pallas kernels  175 us (98%)
  local copies, waits for them, and re-layouts  4.12 us (2%)
    pallas_call x1, Pallas kernels, fast_body(): pl.pallas_call(lambda *refs: kernel(sy_count, *refs), out_shape=jax.Shape...  175 us

profile of v1, /device:TPU:0, one launch (start us, length us, event | category | flops | bytes accessed | tf_op | source)
XLA Modules:
  0.0 178.9 jit_solution(6983607124027445876)
XLA Ops:
  0.0 0.0 copy-start
  0.0 0.0 copy-start.1
  0.0 1.9 %copy.11 = f32[1,2,16,32,256]{4,2,3,1,0:T(8,128)S(1)} copy(f32[1,2,16,32,256]{4,3,2,1,0:T(8,128)} %param.3) | data formatting | bytes 2097152 | tf_op args[0]
  1.9 0.0 copy-done
  1.9 0.0 copy-done.1
  1.9 0.6 copy_bitcast_fusion.1
  2.6 174.7 %shard_map.37 = f32[2,32,16,256]{3,2,1,0:T(8,128)S(1)} custom-call(f32[2,32,16,256]{3,2,1,0:T(8,128)S(1)} %bitcast.12, f32[32,16,256]{2,1,0:T(8,128)S(1)} %get-tuple-element.6.refs_1_, f32[32,16,256]{2,1,0:T(8,128)S(1)} %get-tuple-element.5.refs_2_), custom_call_target="tpu_custom_call" | custom-call | tf_op jit(solution)/shard_map/pallas_call | solution.py:358
  177.3 1.6 copy.7
Async XLA Ops:
  0.0 1.9 %copy-start = (f32[16,32,256]{2,1,0:T(8,128)S(1)}, f32[16,32,256]{2,1,0:T(8,128)}, u32[]{:S(2)}) copy-start(f32[16,32,256]{2,1,0:T(8,128)} %param.5) | copy-start | bytes 1572868
  0.0 1.9 %copy-start.1 = (f32[16,32,256]{2,1,0:T(8,128)S(1)}, f32[16,32,256]{2,1,0:T(8,128)}, u32[]{:S(2)}) copy-start(f32[16,32,256]{2,1,0:T(8,128)} %param.4) | copy-start | bytes 1572868

commit v2 on v1

--- a/solution.py
+++ b/solution.py
@@ -6,7 +6,7 @@
 from jax.sharding import PartitionSpec as P
 
 MESH = pl.DeviceIdType.MESH
-WIDTH = 4
+WIDTH = 12
 CHUNKS = 4
 
 SWEEPS = 2
@@ -206,6 +206,21 @@
         for copy in edge_copies:
             copy.wait_recv()
 
+        def send_halo(e):
+            def stage(y):
+                halo_out[e, 0, y] = xj[0, w + y]
+                halo_out[e, 1, y] = xj[0, ny + y]
+
+            planes(0, w, stage)
+            return [
+                send(halo_out.at[e, 0], halo_in.at[e, 0], down),
+                send(halo_out.at[e, 1], halo_in.at[e, 1], up),
+            ]
+
+        copies = None
+        if sweep > 0:
+            copies = send_halo(exchanges)
+
         def forces(y):
             u, v = x[0, y + 1], x[1, y + 1]
             feed, kill = f_ref[y], k_ref[y]
@@ -256,6 +271,10 @@
                 part_out.at[sweep, :, rows], part_in.at[sweep, :, rows], across
             )
 
+        if sweep == 0:
+            first_pair.wait_recv()
+            copies = send_halo(exchanges)
+
         scale_own = jnp.where(s == 0, scale[0], scale[1])
         scale_other = jnp.where(s == 0, scale[1], scale[0])
 
@@ -263,7 +282,23 @@
             rj[sweep, y + w, own_rows, :] = (local[0, s, y] + part_in[sweep, s, y]) * scale_own
             right_out[sweep, y] = (local[0, other, y] + part_in[sweep, other, y]) * scale_other
 
-        for c in order:
+        near = min(step, w - 1)
+        far = w - 1 - near
+        right_halo = []
+
+        def send_right(low, high, many):
+            right_halo.append(send(
+                rj.at[sweep, pl.ds(w + low, many)], rj.at[sweep, pl.ds(w + ny + low, many)], down
+            ))
+            right_halo.append(send(
+                rj.at[sweep, pl.ds(w + high, many)], rj.at[sweep, pl.ds(w + high - ny, many)], up
+            ))
+
+        for place, c in enumerate(order):
+            if place == 2:
+                for done in order[:2]:
+                    right_copies[done].wait_recv()
+                send_right(0, ny - near, near)
             part_copies[c].wait_recv()
             planes(c * step, (c + 1) * step, rights)
             right_copies[c] = send(
@@ -271,27 +306,15 @@
                 rj.at[sweep, pl.ds(w + c * step, step), own_rows, :],
                 pair,
             )
-        if sweep == 0:
-            first_pair.wait_recv()
-        for c in order[:2]:
+        for c in order[2:]:
             right_copies[c].wait_recv()
-        right_halo = [
-            send(rj.at[sweep, pl.ds(w, w - 1)], rj.at[sweep, pl.ds(w + ny, w - 1)], down),
-            send(rj.at[sweep, pl.ds(w + ny - w + 1, w - 1)], rj.at[sweep, pl.ds(1, w - 1)], up),
-        ]
+        if far:
+            send_right(near, ny - near - far, far)
         for block in range(JACOBI // w):
             e = exchanges
             exchanges += 1
-            for y in range(w):
-                halo_out[e, 0, y] = xj[0, w + y]
-                halo_out[e, 1, y] = xj[0, ny + y]
-            copies = [
-                send(halo_out.at[e, 0], halo_in.at[e, 0], down),
-                send(halo_out.at[e, 1], halo_in.at[e, 1], up),
-            ]
-            if block == 0:
-                for c in order[2:]:
-                    right_copies[c].wait_recv()
+            if block > 0:
+                copies = send_halo(e)
 
             def sweep_planes(turn, first, last):
                 src, dst = (turn - 1) % 2, turn % 2
@@ -312,9 +335,12 @@
             if block == 0:
                 for copy in right_halo:
                     copy.wait_recv()
-            for y in range(w):
+
+            def land(y):
                 xj[0, w + ny + y] = halo_in[e, 0, y]
                 xj[0, y] = halo_in[e, 1, y]
+
+            planes(0, w, land)
             for turn in range(1, w + 1):
                 sweep_planes(turn, turn - w, turn)
                 sweep_planes(turn, ny - turn, ny + w - turn)
@@ -353,7 +379,7 @@
     w = WIDTH
     block = (2, ny, nx, nz)
     blocks = SWEEPS * (JACOBI // w)
-    copies = SWEEPS * (4 + 3 * CHUNKS + 2 + 2 * (JACOBI // w) + 1) + 2
+    copies = SWEEPS * (4 + 3 * CHUNKS + 4 + 2 * (JACOBI // w) + 1) + 2
     vmem = pl.BlockSpec(memory_space=pltpu.VMEM)
     out = pl.pallas_call(
         lambda *refs: kernel(sy_count, *refs),

time: 179 us -> 196 us (1.095)
  Pallas kernels: 175 us -> 192 us
    pallas_call x1, Pallas kernels: 175 us -> 192 us  [fast_body(): pl.pallas_call(lambda *refs: kernel(sy_count, *refs), out_shape=jax.Shape...]
where the time goes in v2:
time: 196 us
  Pallas kernels  192 us (98%)
  local copies, waits for them, and re-layouts  4.12 us (2%)
    pallas_call x1, Pallas kernels, fast_body(): pl.pallas_call(lambda *refs: kernel(sy_count, *refs), out_shape=jax.Shape...  192 us

profile of v2, /device:TPU:0, one launch (start us, length us, event | category | flops | bytes accessed | tf_op | source)
XLA Modules:
  0.0 195.7 jit_solution(16619372524420521660)
XLA Ops:
  0.0 0.0 copy-start
  0.0 0.0 copy-start.1
  0.0 1.9 copy.11
  1.9 0.0 copy-done
  1.9 0.0 copy-done.1
  1.9 0.6 copy_bitcast_fusion.1
  2.6 191.6 %shard_map.37 = f32[2,32,16,256]{3,2,1,0:T(8,128)S(1)} custom-call(f32[2,32,16,256]{3,2,1,0:T(8,128)S(1)} %bitcast.12, f32[32,16,256]{2,1,0:T(8,128)S(1)} %get-tuple-element.6.refs_1_, f32[32,16,256]{2,1,0:T(8,128)S(1)} %get-tuple-element.5.refs_2_), custom_call_target="tpu_custom_call" | custom-call | tf_op jit(solution)/shard_map/pallas_call | solution.py:384
  194.2 1.6 copy.7
Async XLA Ops:
  0.0 1.9 copy-start
  0.0 1.9 copy-start.1

commit v3 on v2

--- a/solution.py
+++ b/solution.py
@@ -8,6 +8,7 @@
 MESH = pl.DeviceIdType.MESH
 WIDTH = 12
 CHUNKS = 4
+GROUP = 4
 
 SWEEPS = 2
 JACOBI = 12
@@ -165,12 +166,25 @@
     other_rows = pl.ds(pl.multiple_of(nx * other, nx), nx)
     row = lax.broadcasted_iota(jnp.int32, (nx, nz), 0)
 
-    def planes(first, last, fn, unroll=1):
-        def go(y, carry):
-            fn(y)
+    def groups(first, last, fn):
+        whole = (last - first) // GROUP
+
+        def go(at, carry):
+            fn(first + at * GROUP, GROUP)
             return carry
-        if last > first:
-            lax.fori_loop(first, last, go, 0, unroll=unroll)
+
+        if whole > 0:
+            lax.fori_loop(0, whole, go, 0)
+        rest = (last - first) - whole * GROUP
+        if rest > 0:
+            fn(first + whole * GROUP, rest)
+
+    def planes(first, last, fn):
+        def some(y, many):
+            for at in range(many):
+                fn(y + at)
+
+        groups(first, last, some)
 
     def load(y):
         for a in range(2):
@@ -319,14 +333,19 @@
             def sweep_planes(turn, first, last):
                 src, dst = (turn - 1) % 2, turn % 2
 
-                def one(y):
-                    value = xj[src, y]
-                    total = xj[src, y - 1] + xj[src, y + 1]
-                    total = total + pltpu.roll(value, 1, 0) + pltpu.roll(value, full - 1, 0)
-                    total = total + pltpu.roll(value, 1, 1) + pltpu.roll(value, nz - 1, 1)
-                    xj[dst, y] = rj[sweep, y] + gain * total
-
-                planes(first + w, last + w, one)
+                def some(y, many):
+                    held = [xj[src, y + at] for at in range(-1, many + 1)]
+                    results = []
+                    for at in range(many):
+                        value = held[at + 1]
+                        total = held[at] + held[at + 2]
+                        total = total + pltpu.roll(value, 1, 0) + pltpu.roll(value, full - 1, 0)
+                        total = total + pltpu.roll(value, 1, 1) + pltpu.roll(value, nz - 1, 1)
+                        results.append(rj[sweep, y + at] + gain * total)
+                    for at in range(many):
+                        xj[dst, y + at] = results[at]
+
+                groups(first + w, last + w, some)
 
             for turn in range(1, w + 1):
                 sweep_planes(turn, turn, ny - turn)

time: 196 us -> 149 us (0.76)
  Pallas kernels: 192 us -> 145 us
    pallas_call x1, Pallas kernels: 192 us -> 145 us  [fast_body(): pl.pallas_call(lambda *refs: kernel(sy_count, *refs), out_shape=jax.Shape...]
where the time goes in v3:
time: 149 us
  Pallas kernels  145 us (97%)
  local copies, waits for them, and re-layouts  4.12 us (3%)
    pallas_call x1, Pallas kernels, fast_body(): pl.pallas_call(lambda *refs: kernel(sy_count, *refs), out_shape=jax.Shape...  145 us

profile of v3, /device:TPU:0, one launch (start us, length us, event | category | flops | bytes accessed | tf_op | source)
XLA Modules:
  0.0 149.3 jit_solution(18401278797771256674)
XLA Ops:
  0.0 0.0 copy-start
  0.0 0.0 copy-start.1
  0.0 1.9 %copy.11 = f32[1,2,16,32,256]{4,2,3,1,0:T(8,128)S(1)} copy(f32[1,2,16,32,256]{4,3,2,1,0:T(8,128)} %param.3) | data formatting | bytes 2097152 | tf_op args[0]
  1.9 0.0 copy-done
  1.9 0.0 copy-done.1
  1.9 0.6 copy_bitcast_fusion.1
  2.6 145.2 %shard_map.37 = f32[2,32,16,256]{3,2,1,0:T(8,128)S(1)} custom-call(f32[2,32,16,256]{3,2,1,0:T(8,128)S(1)} %bitcast.12, f32[32,16,256]{2,1,0:T(8,128)S(1)} %get-tuple-element.6.refs_1_, f32[32,16,256]{2,1,0:T(8,128)S(1)} %get-tuple-element.5.refs_2_), custom_call_target="tpu_custom_call" | custom-call | tf_op jit(solution)/shard_map/pallas_call | solution.py:403
  147.7 1.6 %copy.7 = f32[1,2,16,32,256]{4,3,2,1,0:T(8,128)} copy(f32[1,2,16,32,256]{4,2,3,1,0:T(8,128)S(1)} %bitcast.13) | data formatting | bytes 2097152 | tf_op jit(solution)/shard_map/broadcast_in_dim | solution.py:432
Async XLA Ops:
  0.0 1.9 %copy-start = (f32[16,32,256]{2,1,0:T(8,128)S(1)}, f32[16,32,256]{2,1,0:T(8,128)}, u32[]{:S(2)}) copy-start(f32[16,32,256]{2,1,0:T(8,128)} %param.5) | copy-start | bytes 1572868
  0.0 1.9 %copy-start.1 = (f32[16,32,256]{2,1,0:T(8,128)S(1)}, f32[16,32,256]{2,1,0:T(8,128)}, u32[]{:S(2)}) copy-start(f32[16,32,256]{2,1,0:T(8,128)} %param.4) | copy-start | bytes 1572868

commit v4 on v3

--- a/solution.py
+++ b/solution.py
@@ -324,6 +324,16 @@
             right_copies[c].wait_recv()
         if far:
             send_right(near, ny - near - far, far)
+        backs = []
+
+        def send_back(low, many):
+            source = xj.at[0, pl.ds(w + low, many), other_rows, :]
+            if sweep < SWEEPS - 1:
+                target = xe.at[sweep + 1, s, pl.ds(1 + low, many)]
+            else:
+                target = back.at[pl.ds(low, many)]
+            backs.append((low, many, send(source, target, pair)))
+
         for block in range(JACOBI // w):
             e = exchanges
             exchanges += 1
@@ -349,6 +359,9 @@
 
             for turn in range(1, w + 1):
                 sweep_planes(turn, turn, ny - turn)
+            last_block = block == JACOBI // w - 1
+            if last_block and ny > 2 * w:
+                send_back(w, ny - 2 * w)
             for copy in copies:
                 copy.wait_recv()
             if block == 0:
@@ -362,31 +375,33 @@
             planes(0, w, land)
             for turn in range(1, w + 1):
                 sweep_planes(turn, turn - w, turn)
+            if last_block:
+                send_back(0, w)
+            for turn in range(1, w + 1):
                 sweep_planes(turn, ny - turn, ny + w - turn)
-        source = xj.at[0, pl.ds(w, ny), other_rows, :]
+            if last_block:
+                send_back(ny - w, w)
         if sweep < SWEEPS - 1:
-            copy = send(source, xe.at[sweep + 1, s, pl.ds(1, ny)], pair)
-
             def keep(y):
                 xe[sweep + 1, s, y + 1] = xj[0, y + w, own_rows, :]
 
             planes(0, ny, keep)
-            copy.wait_recv()
-            copy.wait_send()
-            started.pop()
+            for _, _, copy in backs:
+                copy.wait_recv()
+                copy.wait_send()
+                started.pop()
         else:
-            copy = send(source, back, pair)
-
             def keep(y):
                 out_ref[s, y] = xj[0, y + w, own_rows, :]
 
             planes(0, ny, keep)
-            copy.wait_recv()
 
             def finish(y):
                 out_ref[other, y] = back[y]
 
-            planes(0, ny, finish)
+            for low, many, copy in backs:
+                copy.wait_recv()
+                planes(low, low + many, finish)
     for copy in started:
         copy.wait_send()
 
@@ -398,7 +413,7 @@
     w = WIDTH
     block = (2, ny, nx, nz)
     blocks = SWEEPS * (JACOBI // w)
-    copies = SWEEPS * (4 + 3 * CHUNKS + 4 + 2 * (JACOBI // w) + 1) + 2
+    copies = SWEEPS * (4 + 3 * CHUNKS + 4 + 2 * (JACOBI // w) + 3) + 2
     vmem = pl.BlockSpec(memory_space=pltpu.VMEM)
     out = pl.pallas_call(
         lambda *refs: kernel(sy_count, *refs),

time: 149 us -> 136 us (0.913)
  Pallas kernels: 145 us -> 131 us
    pallas_call x1, Pallas kernels: 145 us -> 131 us  [fast_body(): pl.pallas_call(lambda *refs: kernel(sy_count, *refs), out_shape=jax.Shape...]
where the time goes in v4:
time: 136 us; the launch traced here: 135 us
  Pallas kernels  131 us (96%)
  local copies, waits for them, and re-layouts  4.12 us (3%)
    pallas_call x1, Pallas kernels, fast_body(): pl.pallas_call(lambda *refs: kernel(sy_count, *refs), out_shape=jax.Shape...  131 us

profile of v4, /device:TPU:0, one launch (start us, length us, event | category | flops | bytes accessed | tf_op | source)
XLA Modules:
  0.0 135.2 jit_solution(17394055922915560650)
XLA Ops:
  0.0 0.0 copy-start
  0.0 0.0 copy-start.1
  0.0 1.9 %copy.11 = f32[1,2,16,32,256]{4,2,3,1,0:T(8,128)S(1)} copy(f32[1,2,16,32,256]{4,3,2,1,0:T(8,128)} %param.3) | data formatting | bytes 2097152 | tf_op args[0]
  1.9 0.0 copy-done
  1.9 0.0 copy-done.1
  1.9 0.6 copy_bitcast_fusion.1
  2.6 131.1 %shard_map.37 = f32[2,32,16,256]{3,2,1,0:T(8,128)S(1)} custom-call(f32[2,32,16,256]{3,2,1,0:T(8,128)S(1)} %bitcast.12, f32[32,16,256]{2,1,0:T(8,128)S(1)} %get-tuple-element.6.refs_1_, f32[32,16,256]{2,1,0:T(8,128)S(1)} %get-tuple-element.5.refs_2_), custom_call_target="tpu_custom_call" | custom-call | tf_op jit(solution)/shard_map/pallas_call | solution.py:418
  133.7 1.6 %copy.7 = f32[1,2,16,32,256]{4,3,2,1,0:T(8,128)} copy(f32[1,2,16,32,256]{4,2,3,1,0:T(8,128)S(1)} %bitcast.13) | data formatting | bytes 2097152 | tf_op jit(solution)/shard_map/broadcast_in_dim | solution.py:447
Async XLA Ops:
  0.0 1.9 %copy-start = (f32[16,32,256]{2,1,0:T(8,128)S(1)}, f32[16,32,256]{2,1,0:T(8,128)}, u32[]{:S(2)}) copy-start(f32[16,32,256]{2,1,0:T(8,128)} %param.5) | copy-start | bytes 1572868
  0.0 1.9 %copy-start.1 = (f32[16,32,256]{2,1,0:T(8,128)S(1)}, f32[16,32,256]{2,1,0:T(8,128)}, u32[]{:S(2)}) copy-start(f32[16,32,256]{2,1,0:T(8,128)} %param.4) | copy-start | bytes 1572868
